TPU v7x, 256 devices: a whole 4x4x8 slice. The times are simulated.
256 devices in a mesh: img: 4 (over x), seq: 8 (over z_lo, y), tp: 8 (over z_hi, core).
Axes of the slice: x: 4, y: 4, z: 8 (z_hi: 4, z_lo: 2; z = z_hi * 2 + z_lo), core: 2. Of those that a mesh axis runs over, the one named last changes fastest.
Arguments:
- vit_qkv: bfloat16 [4, 4096, 3, 1280], P('img', ('seq', 'tp')), may hold values from -6 to 6
- patch_counts: int32 [4], P('img'), may hold values from 1024 to 4096, as said below
- vit_out_weight: bfloat16 [1280, 1280], replicated, may hold values from -0.15625 to 0.15625
- vit_norm_gain: float32 [1280], replicated, may hold values from 0.25 to 1.75
- merger_weight: bfloat16 [5120, 8192], P(('img', 'seq'), 'tp'), may hold values from -8 to 8
- lm_norm_gain: float32 [8192], P('tp'), may hold values from 0.25 to 1.75
- kv_weight: bfloat16 [8192, 2048], P('tp', ('img', 'seq')), may hold values from -0.0625 to 0.0625
- queries: bfloat16 [4, 4096, 64, 128], P('img', 'seq', 'tp'), may hold values from -6 to 6
- span_kv: bfloat16 [4, 4096, 2, 8, 128], P('img', 'seq', None, 'tp'), may hold values from -6 to 6
Outputs:
- lm_attention: bfloat16 [4, 4096, 64, 128], P('img', 'seq', 'tp')
Inputs may be any that keep to these rules, and one draw needn't show every extreme that they name: `patch_counts`: each count is a multiple of 4, at least 1024, and some image has exactly 4096.
All inputs are finite; a program needn't handle non-finite values.
Results may differ from a plain program's by a relative error of at most 0.04.
Values may be sent and summed in bfloat16 or wider, within the bound.
A program may use at most 128 MiB of HBM per device.

v0:
```python
import jax
import jax.numpy as jnp
from jax import lax
from jax.sharding import Mesh
from jax.sharding import PartitionSpec as P

VIT_D = 1280
VIT_HEADS = 16
VIT_HDIM = 80
D = 8192
HQ = 64
KVH = 8
HD = 128
SEQ = ("seq_0", "seq_1")
IMG_SEQ = ("img", "seq_0", "seq_1")
SEQ_TP = ("seq_0", "seq_1", "tp")
masked_score = -1e30


def sent_to_all(x, axis):
    copies = jnp.broadcast_to(x, (lax.axis_size(axis), *x.shape))
    return lax.all_to_all(copies, axis, split_axis=0, concat_axis=0, tiled=True)


def in_order(parts, dim):
    parts = jnp.moveaxis(parts, 0, dim)
    lengths = parts.shape
    return parts.reshape(*lengths[:dim], lengths[dim] * lengths[dim + 1], *lengths[dim + 2 :])


def gather_directly(x, axis, dim):
    parts = sent_to_all(x, axis)
    return in_order(parts, dim)


def in_one_piece(arrays, axis, dim, along):
    ends, at = ([], 0)
    for a in arrays[:-1]:
        at += a.shape[along]
        ends.append(at)
    both = jnp.concatenate(arrays, axis=along)
    return tuple(jnp.split(gather_directly(both, axis, dim), ends, axis=along))


def all_blocks(x, axes, sequence):
    parts = x[None]
    for k in sequence:
        parts = lax.all_gather(parts, axes[k], axis=0, tiled=True)
    current = [lax.axis_size(axes[k]) for k in reversed(sequence)]
    parts = parts.reshape(*current, *x.shape)
    turned = sorted(range(len(sequence)), key=lambda place: sequence[len(sequence) - 1 - place])
    return parts.transpose(*turned, *range(len(sequence), parts.ndim)).reshape(-1, *x.shape)


def gathered_by_axis(x, axes, sequence, dim):
    return in_order(all_blocks(x, axes, sequence), dim)


def over_copies(x, axis):
    return sent_to_all(x, axis).sum(axis=0)


def in_blocks(x, dim, length):
    before, after = (x.shape[:dim], x.shape[dim + 1 :])
    return jnp.moveaxis(x.reshape(*before, length, -1, *after), dim, 0)


def sum_at_owner(x, axis, dim):
    length = lax.axis_size(axis)
    parts = lax.all_to_all(in_blocks(x, dim, length), axis, 0, 0, tiled=True)
    return jnp.sum(parts.astype(jnp.float32), axis=0)


def in_one_piece_2(arrays, axis, dim, along):
    widths = [a.shape[along] for a in arrays]
    both = jnp.concatenate(arrays, axis=along)
    out = lax.all_gather(both, axis, axis=dim, tiled=True)
    return tuple(jnp.split(out, [sum(widths[:k]) for k in range(1, len(widths))], axis=along))


def fold_block(running, scores, usable, value_block, forms):
    peak, weight_sum, blended = running
    scores = jnp.where(usable, scores, masked_score)
    new_peak = jnp.maximum(peak, jnp.max(scores, axis=-1))
    weights = jnp.where(usable, jnp.exp(scores - new_peak[..., None]), 0.0)
    decay = jnp.exp(peak - new_peak)
    weight_sum = weight_sum * decay + jnp.sum(weights, axis=-1)
    blended = blended * decay[..., None] + jnp.einsum(
        forms, weights.astype(jnp.bfloat16), value_block, preferred_element_type=jnp.float32
    )
    return (new_peak, weight_sum, blended)


def local(
    vit_qkv,
    patch_counts,
    vit_out_weight,
    vit_norm_gain,
    merger_weight,
    lm_norm_gain,
    kv_weight,
    queries,
    span_kv,
):
    patch_rows = vit_qkv.shape[1]
    tp_count = lax.axis_size("tp")
    seq_index = lax.axis_index(SEQ)
    tp_index = lax.axis_index("tp")
    patch_total = patch_counts[0]
    local_qkv = vit_qkv[0].reshape(patch_rows, 3, VIT_HEADS, VIT_HDIM)
    scaling = VIT_HDIM ** (-0.5)
    spread = lax.all_to_all(local_qkv, SEQ, split_axis=2, concat_axis=0, tiled=True)
    local_rows = spread.shape[0]

    def seq_rows(index):
        source = index // local_rows
        within = index % local_rows
        return (within // patch_rows * tp_count + source) * patch_rows + within % patch_rows

    heads_local = spread.shape[2]
    query_count = spread.shape[0]
    query_rows = spread[:, 0]
    running = (
        jnp.full((heads_local, query_count), masked_score, jnp.float32),
        jnp.zeros((heads_local, query_count), jnp.float32),
        jnp.zeros((heads_local, query_count, VIT_HDIM), jnp.float32),
    )
    make_heads_local = query_rows.shape[1]
    key_piece, value_piece = in_one_piece((spread[:, 1], spread[:, 2]), "tp", 0, 1)
    blocks = key_piece.shape[0] // local_rows
    key_blocks = key_piece.reshape(blocks, local_rows, make_heads_local, VIT_HDIM)
    value_blocks = value_piece.reshape(blocks, local_rows, make_heads_local, VIT_HDIM)
    offsets = jnp.arange(blocks, dtype=jnp.int32) * local_rows

    def make_advance(state, inputs):
        key_block, value_block, offset = inputs
        usable = seq_rows(offset + jnp.arange(local_rows, dtype=jnp.int32)) < patch_total
        scores = (
            jnp.einsum("qhd,khd->hqk", query_rows, key_block, preferred_element_type=jnp.float32)
            * scaling
        )
        return (fold_block(state, scores, usable[None, None, :], value_block, "hqk,khd->hqd"), None)

    result, _ = lax.scan(make_advance, running, (key_blocks, value_blocks, offsets))
    state = result
    peak, weight_sum, blended = state
    returned = lax.all_to_all(
        jnp.transpose(blended / weight_sum[..., None], (1, 0, 2)).astype(jnp.bfloat16),
        SEQ,
        split_axis=0,
        concat_axis=1,
        tiled=True,
    )
    attended = returned.reshape(patch_rows, VIT_D)
    hidden = jnp.dot(attended, vit_out_weight, preferred_element_type=jnp.float32)
    patch_ids = (seq_index * tp_count + tp_index) * patch_rows + jnp.arange(
        patch_rows, dtype=jnp.int32
    )
    hidden = jnp.where((patch_ids < patch_total)[:, None], hidden, 0.0)
    centred = hidden - jnp.mean(hidden, axis=-1, keepdims=True)
    spread_sq = jnp.mean(centred * centred, axis=-1, keepdims=True)
    normed = (centred * lax.rsqrt(spread_sq + 1e-06) * vit_norm_gain).astype(jnp.bfloat16)
    merged_local = normed.reshape(patch_rows // 4, 4 * VIT_D)
    token_rows = gather_directly(merged_local, "tp", 0)
    embedded_sum = jnp.dot(
        token_rows,
        gathered_by_axis(merger_weight, IMG_SEQ, (1, 0, 2), 0),
        preferred_element_type=jnp.float32,
    )
    embedded = lax.optimization_barrier(embedded_sum.astype(jnp.bfloat16))
    embedded_wide = embedded.astype(jnp.float32)
    square_sums = over_copies(jnp.sum(embedded_wide * embedded_wide, axis=-1), "tp")
    lm_normed = (embedded_wide * lax.rsqrt(square_sums[:, None] / D + 1e-06) * lm_norm_gain).astype(
        jnp.bfloat16
    )
    kv_terms = jnp.dot(
        lm_normed,
        lax.all_gather(kv_weight, IMG_SEQ, axis=1, tiled=True),
        preferred_element_type=jnp.float32,
    )
    visual_count = kv_terms.shape[0]
    kv_terms = kv_terms.reshape(visual_count, 2, KVH, HD)
    visual_kv = sum_at_owner(kv_terms.astype(jnp.bfloat16), "tp", 2).astype(jnp.bfloat16)
    span_rows = queries.shape[1]
    kv_local = span_kv.shape[3]
    groups = HQ // KVH
    lm_scaling = HD ** (-0.5)
    grouped = queries[0].reshape(span_rows, kv_local, groups, HD)
    causal = jnp.arange(span_rows)[:, None] >= jnp.arange(span_rows)[None, :]
    near_scores = (
        jnp.einsum("ckgd,nkd->kgcn", grouped, span_kv[0, :, 0], preferred_element_type=jnp.float32)
        * lm_scaling
    )
    initial = (
        jnp.full((kv_local, groups, span_rows), masked_score, jnp.float32),
        jnp.zeros((kv_local, groups, span_rows), jnp.float32),
        jnp.zeros((kv_local, groups, span_rows, HD), jnp.float32),
    )
    initial = fold_block(
        initial, near_scores, causal[None, None], span_kv[0, :, 1], "kgcn,nkd->kgcd"
    )
    visual_total = patch_total // 4
    key_piece, value_piece = in_one_piece_2((visual_kv[:, 0], visual_kv[:, 1]), SEQ, 0, 1)
    blocks = key_piece.shape[0] // visual_count
    key_blocks = key_piece.reshape(blocks, visual_count, kv_local, HD)
    value_blocks = value_piece.reshape(blocks, visual_count, kv_local, HD)
    offsets = jnp.arange(blocks, dtype=jnp.int32) * visual_count

    def visual_advance(state, inputs):
        key_block, value_block, offset = inputs
        usable = offset + jnp.arange(visual_count, dtype=jnp.int32) < visual_total
        scores = (
            jnp.einsum("ckgd,nkd->kgcn", grouped, key_block, preferred_element_type=jnp.float32)
            * lm_scaling
        )
        return (
            fold_block(state, scores, usable[None, None, None, :], value_block, "kgcn,nkd->kgcd"),
            None,
        )

    result, _ = lax.scan(visual_advance, initial, (key_blocks, value_blocks, offsets))
    peak, weight_sum, blended = result
    result = jnp.transpose(blended / weight_sum[..., None], (2, 0, 1, 3))
    return result.reshape(span_rows, kv_local * groups, HD).astype(jnp.bfloat16)[None]


def solution(mesh):
    torus = Mesh(
        mesh.devices.reshape(mesh.shape["img"], 2, 4, mesh.shape["tp"]),
        ("img", "seq_0", "seq_1", "tp"),
    )
    placed = (
        P("img", SEQ_TP, None, None),
        P("img"),
        P(),
        P(),
        P(IMG_SEQ, "tp"),
        P("tp"),
        P("tp", IMG_SEQ),
        P("img", SEQ, "tp", None),
        P("img", SEQ, None, "tp", None),
    )
    return jax.shard_map(
        local, mesh=torus, in_specs=placed, out_specs=P("img", SEQ, "tp", None), check_vma=False
    )
```

profile of v0, /device:TPU:14, one launch (start us, length us, event | category | flops | bytes accessed | tf_op | source)
XLA Modules:
  0.0 454.1 jit_solution(11617065756509815237)
XLA Ops:
  6.5 12.6 %all-gather = bf16[320,1024]{1,0:T(8,128)(2,1)} all-gather(bf16[160,1024]{1,0:T(8,128)(2,1)} %param.17), channel_id=2, replica_groups=mesh['img'=4,'seq_0'=2,'seq_1'=4,'tp'=8] {'seq_0'}, dimensions={0}, use_global_device_ids=true | all-gather | bytes 983040 | tf_op jit(solution)/shard_map/all_gather | solution.py:48
  19.2 37.9 %all-gather.5.cloned.1.call-done = bf16[8,160,1024]{2,1,0:T(8,128)(2,1)} async-done(((bf16[2,160,1024]{2,1,0:T(8,128)(2,1)}), bf16[8,160,1024]{2,1,0:T(8,128)(2,1)}) %all-gather.5.cloned.1.call-update) | async-done | bytes 2621456 | tf_op jit(solution)/shard_map/all_gather | solution.py:48
  57.1 2.8 reshape_squeeze.6
  61.3 16.7 %all_to_all.54 = bf16[64,3,16,80]{3,0,1,2:T(8,128)(2,1)} all-to-all(bf16[64,3,16,80]{3,0,1,2:T(8,128)(2,1)S(1)} %copy.154), channel_id=1, replica_groups=mesh['img'=4,'seq_0'=2,'seq_1'=4,'tp'=8] {'seq_0','seq_1'}, dimensions={2} | all-to-all | bytes 983040 | tf_op jit(solution)/shard_map/all_to_all | solution.py:112
  77.9 2.4 copy.156
  80.3 2.6 all_to_all.40
  85.8 6.1 %all-to-all-start.1 = ((bf16[8,512,4,80]{1,3,2,0:T(8,128)(2,1)}), bf16[8,512,4,80]{1,3,2,0:T(8,128)(2,1)}, u32[]{:S(2)}, u32[]{:S(2)}) async-start(bf16[8,512,4,80]{1,3,2,0:T(8,128)(2,1)} %broadcast_in_dim.148), calls=%async_computation.1 | async-start | bytes 5242880 | tf_op jit(solution)/shard_map/all_to_all | solution.py:22
  92.6 62.4 %all-to-all-done.1 = bf16[8,512,4,80]{1,3,2,0:T(8,128)(2,1)} async-done(((bf16[8,512,4,80]{1,3,2,0:T(8,128)(2,1)}), bf16[8,512,4,80]{1,3,2,0:T(8,128)(2,1)}, u32[]{:S(2)}, u32[]{:S(2)}) %all-to-all-start.1) | async-done | bytes 2621472 | tf_op jit(solution)/shard_map/all_to_all | solution.py:22
  159.1 76.2 %while.33 = (s32[]{:T(128)}, f32[2,512]{1,0:T(2,128)S(1)}, f32[2,512]{1,0:T(2,128)S(1)}, f32[2,512,80]{1,2,0:T(8,128)}, s32[8]{0:T(128)S(1)}, /*index=5*/s32[]{:...) while((s32[]{:T(128)}, f32[2,512]{1,0:T(2,128)S(1)}, ...), condition=%wide.region_5.6_spmd.clone, body=%wide.region_2.5_spmd.clone.sunk | while | flops 174861312 | bytes 15896233 | solution.py:144
  161.0 2.8 bitcast_reduce_fusion.5
  166.1 2.4 convolution_add_fusion.2
  170.4 2.7 bitcast_reduce_fusion.5
  175.5 2.5 convolution_add_fusion.2
  180.0 2.7 bitcast_reduce_fusion.5
  182.7 2.3 fusion.110
  185.1 2.5 convolution_add_fusion.2
  189.5 2.7 bitcast_reduce_fusion.5
  192.2 2.3 fusion.110
  194.6 2.5 convolution_add_fusion.2
  199.0 2.8 bitcast_reduce_fusion.5
  201.8 2.3 fusion.110
  204.2 2.5 convolution_add_fusion.2
  208.6 2.7 bitcast_reduce_fusion.5
  211.4 2.3 fusion.110
  213.7 2.5 convolution_add_fusion.2
  218.1 2.7 bitcast_reduce_fusion.5
  223.3 2.5 convolution_add_fusion.2
  227.7 2.8 bitcast_reduce_fusion.5
  230.4 2.3 fusion.110
  232.8 2.5 convolution_add_fusion.2
  237.2 4.3 all-to-all-start.2
  242.2 6.0 %all-to-all-done.2 = bf16[512,2,80]{2,1,0:T(2,128)(2,1)S(1)} async-done(((bf16[512,2,80]{2,1,0:T(2,128)(2,1)}), bf16[512,2,80]{2,1,0:T(2,128)(2,1)S(1)}, u32[]{:S(2)}, u32[]{:S(2)}) %all-to-all-start.2) | async-done | bytes 163872 | tf_op jit(solution)/shard_map/all_to_all | solution.py:147
  254.8 3.9 all-to-all-start.3
  259.8 4.9 %fusion.55 = (f32[8,512]{1,0:T(8,128)S(1)}, f32[512,512,8]{1,0,2:T(8,128)}) fusion(pred[512,512]{0,1:T(8,128)(4,1)S(1)} %iota_compare_fusion, bf16[512,8,128]{2,1,0:T(8,128)(2,1)S(1)} %bitcast.250, bf16[1,512,1,1,128]{4,2,3,1,0:T(2,128)(2,1)S(1)} %get-tuple-element.403), kind=kOutput, calls=%fused_computation.84 | convolution fusion | flops 543158272 | bytes 9846784 | tf_op jit(solution)/shard_map/ckgd,nkd->kgcn/dot_general | solution.py:191
  264.8 9.9 %copy.165 = bf16[4,2,4,160,1024]{4,3,2,1,0:T(8,128)(2,1)} copy(bf16[4,2,4,160,1024]{4,3,1,0,2:T(8,128)(2,1)} %bitcast.243) | data formatting | bytes 20971520 | tf_op jit(solution)/shard_map/transpose | solution.py:52
  274.7 18.9 %all-to-all-done.3 = bf16[8,16,5120]{2,1,0:T(8,128)(2,1)S(1)} async-done(((bf16[8,16,5120]{2,1,0:T(8,128)(2,1)}), bf16[8,16,5120]{2,1,0:T(8,128)(2,1)S(1)}, u32[]{:S(2)}, u32[]{:S(2)}) %all-to-all-start.3) | async-done | bytes 1310752 | tf_op jit(solution)/shard_map/all_to_all | solution.py:22
  293.6 5.5 %convolution_convert_fusion.1 = bf16[128,1024]{1,0:T(8,128)(2,1)S(1)} fusion(bf16[128,5120]{1,0:T(8,128)(2,1)S(1)} %bitcast.247, bf16[5120,1024]{1,0:T(8,128)(2,1)} %bitcast.241), kind=kOutput, calls=%fused_computation.98 | convolution fusion | flops 1342308352 | bytes 12058624 | tf_op jit(solution)/shard_map/dot_general | solution.py:165
  299.9 3.3 all-to-all-start.4
  303.2 4.5 fusion.57
  307.7 3.0 all-to-all-done.4
  310.8 17.5 %all-gather.9.cloned.1.call-done = bf16[1024,2048]{0,1:T(8,128)(2,1)} async-done(((bf16[1024,64]{0,1:T(8,128)(2,1)}), bf16[1024,2048]{0,1:T(8,128)(2,1)}) %all-gather.9.cloned.1.call-update) | async-done | bytes 4194320 | tf_op jit(solution)/shard_map/all_gather | solution.py:178
  328.3 3.7 fusion.65
  333.3 5.1 %all-to-all-start.5 = ((bf16[8,128,2,1,128]{4,2,1,3,0:T(2,128)(2,1)}), bf16[8,128,2,1,128]{4,2,1,3,0:T(2,128)(2,1)}, u32[]{:S(2)}, u32[]{:S(2)}) async-start(bf16[8,128,2,1,128]{4,2,1,3,0:T(2,128)(2,1)} %bitcast.189), calls=%async_computation.5 | async-start | bytes 1048576 | tf_op jit(solution)/shard_map/all_to_all | solution.py:70
  338.6 7.4 %add_bitcast_fusion = f32[1,8,512,128]{3,2,1,0:T(8,128)} fusion(f32[512,512,8]{1,0,2:T(8,128)} %get-tuple-element.412, f32[8,512]{1,0:T(8,128)S(1)} %get-tuple-element.408, pred[512,512]{0,1:T(8,128)(4,1)S(1)} %iota_compare_fusion, f32[8,512]{1,0:T(8,128)S(1)} %get-tuple-element.406, bf16[1,512,1,1,128]{4,2,3,1,0:T(2,128)(2,1)S(1)} %copy-done.7), kind=kOutput, calls=%fused_computation.94 | convolution fusion | flops 547880960 | bytes 10911744 | tf_op jit(solution)/shard_map/kgcn,nkd->kgcd/dot_general | solution.py:88
  346.0 10.9 %all-to-all-done.5 = bf16[8,128,2,1,128]{4,2,1,3,0:T(2,128)(2,1)} async-done(((bf16[8,128,2,1,128]{4,2,1,3,0:T(2,128)(2,1)}), bf16[8,128,2,1,128]{4,2,1,3,0:T(2,128)(2,1)}, u32[]{:S(2)}, u32[]{:S(2)}) %all-to-all-start.5) | async-done | bytes 524320 | tf_op jit(solution)/shard_map/all_to_all | solution.py:70
  358.6 34.6 %all_gather.19 = bf16[1024,2,128]{2,0,1:T(8,128)(2,1)S(1)} all-gather(bf16[128,2,128]{2,0,1:T(8,128)(2,1)S(1)} %pad_maximum_fusion.1), channel_id=1, replica_groups=mesh['img'=4,'seq_0'=2,'seq_1'=4,'tp'=8] {'seq_0','seq_1'}, dimensions={0}, use_global_device_ids=true | all-gather | bytes 589824 | tf_op jit(solution)/shard_map/all_gather | solution.py:77
  393.9 49.6 %while.32 = (s32[]{:T(128)}, f32[1,8,512]{2,1,0:T(8,128)S(1)}, f32[1,8,512]{2,1,0:T(8,128)S(1)}, f32[1,8,512,128]{3,2,1,0:T(8,128)}, s32[8]{0:T(128)S(1)}, /*ind...) while((s32[]{:T(128)}, f32[1,8,512]{2,1,0:T(8,128)S(1)}, ...), condition=%wide.region_14.15_spmd, body=%wide.region_11.14_spmd.sunk | while | flops 276312320 | bytes 28641840 | solution.py:221
  443.7 3.9 fusion.68
  (219 shorter events, 95.1 us)
Async XLA Ops:
  6.5 244.8 %copy-start = (bf16[1280,1280]{1,0:T(8,128)(2,1)S(1)}, bf16[1280,1280]{1,0:T(8,128)(2,1)}, u32[]{:S(2)}) copy-start(bf16[1280,1280]{1,0:T(8,128)(2,1)} %param.15) | copy-start | bytes 9830404
  6.5 50.6 %all-gather.5.cloned.1.call-start = ((), (), s32[]{:S(2)}) async-start(), calls=%async_computation.6 | async-start | bytes 3276800 | tf_op jit(solution)/shard_map/all_gather | solution.py:48
  19.1 245.6 %all-gather.7.cloned.1.call-start = ((), (), s32[]{:S(2)}) async-start(), calls=%async_computation.7 | async-start | bytes 13107200 | tf_op jit(solution)/shard_map/all_gather | solution.py:48
  85.8 69.3 %all-to-all-start.1 = ((bf16[8,512,4,80]{1,3,2,0:T(8,128)(2,1)}), bf16[8,512,4,80]{1,3,2,0:T(8,128)(2,1)}, u32[]{:S(2)}, u32[]{:S(2)}) async-start(bf16[8,512,4,80]{1,3,2,0:T(8,128)(2,1)} %broadcast_in_dim.148), calls=%async_computation.1 | async-start | bytes 5242880 | tf_op jit(solution)/shard_map/all_to_all | solution.py:22
  91.9 236.4 %all-gather.9.cloned.1.call-start = ((), (), s32[]{:S(2)}) async-start(), calls=%async_computation.8 | async-start | bytes 4325376 | tf_op jit(solution)/shard_map/all_gather | solution.py:178
  163.8 2.4 copy-start.2
  173.2 2.4 copy-start.2
  182.7 2.4 copy-start.2
  192.2 2.4 copy-start.2
  201.8 2.4 copy-start.2
  211.3 2.4 copy-start.2
  220.9 2.4 copy-start.2
  230.4 2.4 copy-start.2
  237.2 10.9 %all-to-all-start.2 = ((bf16[512,2,80]{2,1,0:T(2,128)(2,1)}), bf16[512,2,80]{2,1,0:T(2,128)(2,1)S(1)}, u32[]{:S(2)}, u32[]{:S(2)}) async-start(bf16[512,2,80]{2,1,0:T(2,128)(2,1)} %bitcast.256), calls=%async_computation.2 | async-start | bytes 524288 | tf_op jit(solution)/shard_map/all_to_all | solution.py:147
  251.3 2.0 copy-start.8
  253.5 5.2 %copy-start.6 = (bf16[1,512,2,1,128]{4,2,3,1,0:T(2,128)(2,1)S(1)}, bf16[1,512,2,1,128]{4,2,3,1,0:T(2,128)(2,1)}, u32[]{:S(2)}) copy-start(bf16[1,512,2,1,128]{4,2,3,1,0:T(2,128)(2,1)} %param.21) | copy-start | bytes 786436
  254.8 5.1 %copy-start.5 = (bf16[1,512,8,128]{3,2,1,0:T(8,128)(2,1)S(1)}, bf16[1,512,8,128]{3,2,1,0:T(8,128)(2,1)}, u32[]{:S(2)}) copy-start(bf16[1,512,8,128]{3,2,1,0:T(8,128)(2,1)} %param.20) | copy-start | bytes 3145732
  254.8 38.8 %all-to-all-start.3 = ((bf16[8,16,5120]{2,1,0:T(8,128)(2,1)}), bf16[8,16,5120]{2,1,0:T(8,128)(2,1)S(1)}, u32[]{:S(2)}, u32[]{:S(2)}) async-start(bf16[8,16,5120]{2,1,0:T(8,128)(2,1)} %broadcast_in_dim.150), calls=%async_computation.3 | async-start | bytes 2621440 | tf_op jit(solution)/shard_map/all_to_all | solution.py:22
  299.9 10.9 %all-to-all-start.4 = ((f32[8,1,128]{2,1,0:T(1,128)}), f32[8,1,128]{2,1,0:T(1,128)S(1)}, u32[]{:S(2)}, u32[]{:S(2)}) async-start(f32[8,1,128]{2,1,0:T(1,128)} %broadcast_in_dim.152), calls=%async_computation.4 | async-start | bytes 8192 | tf_op jit(solution)/shard_map/all_to_all | solution.py:22
  303.2 25.1 %copy-start.9 = (f32[1024]{0:T(1024)S(1)}, f32[1024]{0:T(1024)}, u32[]{:S(2)}) copy-start(f32[1024]{0:T(1024)} %param.18) | copy-start | bytes 12292
  332.1 6.5 %copy-start.7 = (bf16[1,512,1,1,128]{4,2,3,1,0:T(2,128)(2,1)S(1)}, bf16[1,512,1,1,128]{4,2,3,1,0:T(2,128)(2,1)}, u32[]{:S(2)}) copy-start(bf16[1,512,1,1,128]{4,2,3,1,0:T(2,128)(2,1)} %get-tuple-element.402) | copy-start | bytes 393220
  333.3 23.6 %all-to-all-start.5 = ((bf16[8,128,2,1,128]{4,2,1,3,0:T(2,128)(2,1)}), bf16[8,128,2,1,128]{4,2,1,3,0:T(2,128)(2,1)}, u32[]{:S(2)}, u32[]{:S(2)}) async-start(bf16[8,128,2,1,128]{4,2,1,3,0:T(2,128)(2,1)} %bitcast.189), calls=%async_computation.5 | async-start | bytes 1048576 | tf_op jit(solution)/shard_map/all_to_all | solution.py:70
  393.9 2.5 copy-start.3
  398.8 1.3 copy-start.4
  400.1 2.6 copy-start.3
  405.0 1.3 copy-start.4
  406.3 2.6 copy-start.3
  411.2 1.3 copy-start.4
  412.5 2.6 copy-start.3
  417.4 1.3 copy-start.4
  418.7 2.6 copy-start.3
  423.6 1.3 copy-start.4
  424.9 2.6 copy-start.3
  429.7 1.3 copy-start.4
  431.1 2.6 copy-start.3
  435.9 1.3 copy-start.4
  437.3 2.6 copy-start.3
  442.1 1.3 copy-start.4
  443.5 4.0 copy-start.1
Sparse Core Ops, SparseCore 0:
  19.3 37.7 all-gather.4
  58.9 105.2 all-gather.6
  166.0 162.2 all-gather.8
where the time goes:
time: 457 us; the launch traced here: 454 us
  waiting for transfers between devices  157 us (34%)
  matrix products  92.9 us (20%)
  blocking collectives  63.8 us (14%)
  local copies, waits for them, and re-layouts  51.3 us (11%)
  other arithmetic  51.2 us (11%)
  starting transfers between devices  22.7 us (5%)
  between operations  14.1 us (3%)
    all_to_all x3, waiting for transfers between devices, sent_to_all(): return lax.all_to_all(copies, axis, split_axis=0, concat_axis=0, tiled=True)  84.3 us
    dot_general x17, matrix products, fold_block(): jnp.einsum(forms, weights.astype(jnp.bfloat16), value_block, preferred_el...  45.3 us
    all_gather x2, waiting for transfers between devices, all_blocks(): parts = lax.all_gather(parts, axes[k], axis=0, tiled=True)  37.9 us
    all_gather x1, blocking collectives, in_one_piece_2(): out = lax.all_gather(both, axis, axis=dim, tiled=True)  34.6 us
    reduce_sum x17, other arithmetic, fold_block(): weight_sum = weight_sum * decay + jnp.sum(weights, axis=-1)  28.1 us
    dot_general x8, matrix products, make_advance(): jnp.einsum('qhd,khd->hqk', query_rows, key_block, preferred_element_type=...  22 us
    all_gather x1, waiting for transfers between devices, local(): lax.all_gather(kv_weight, IMG_SEQ, axis=1, tiled=True)  17.5 us
    all_to_all x1, blocking collectives, local(): lax.all_to_all(local_qkv, SEQ, split_axis=2, concat_axis=0, tiled=True)  16.7 us
  transfers between devices with their start and end apart: 8, of which 7 were waited for; matrix products, arithmetic and copies ran while one was open for 29% of the time, Pallas kernels for 0%

commit v1 on v0

--- a/solution.py
+++ b/solution.py
@@ -45,7 +45,9 @@
 def all_blocks(x, axes, sequence):
     parts = x[None]
     for k in sequence:
-        parts = lax.all_gather(parts, axes[k], axis=0, tiled=True)
+        parts = jnp.concatenate(
+            lax.all_to_all(jnp.stack([parts] * lax.axis_size(axes[k])), axes[k], 0, 0), axis=0
+        )
     current = [lax.axis_size(axes[k]) for k in reversed(sequence)]
     parts = parts.reshape(*current, *x.shape)
     turned = sorted(range(len(sequence)), key=lambda place: sequence[len(sequence) - 1 - place])

time: 457 us -> 579 us (1.27)
  waiting for transfers between devices: 157 us -> 252 us
  blocking collectives: 63.8 us -> 40.7 us
  starting transfers between devices: 22.7 us -> 45.3 us
  local copies, waits for them, and re-layouts: 51.3 us -> 70.3 us
  other arithmetic: 51.2 us -> 64.2 us
    all_to_all x1 -> x4, waiting for transfers between devices: 5.97 us -> 158 us  [the longest x3 149 us: all_blocks(): lax.all_to_all(jnp.stack([parts] * lax.axis_size(axes[k])), axes[k], 0, 0)]
    all_gather x2 -> x0, waiting for transfers between devices: 37.9 us -> none  [all_blocks(): parts = lax.all_gather(parts, axes[k], axis=0, tiled=True)]
    all_to_all x1 -> x4, starting transfers between devices: 4.28 us -> 23.3 us  [the longest x3 17 us: all_blocks(): lax.all_to_all(jnp.stack([parts] * lax.axis_size(axes[k])), axes[k], 0, 0)]
    all_gather x1, waiting for transfers between devices: 17.5 us -> 0.01 us  [local(): lax.all_gather(kv_weight, IMG_SEQ, axis=1, tiled=True)]
    all_gather x1 -> x0, blocking collectives: 12.6 us -> none  [all_blocks(): parts = lax.all_gather(parts, axes[k], axis=0, tiled=True)]
    add x17, other arithmetic: 0.26 us -> 11.4 us  [fold_block(): weight_sum = weight_sum * decay + jnp.sum(weights, axis=-1)]
    another operation x0 -> x2, local copies, waits for them, and re-layouts: none -> 10 us  [all_blocks(): jnp.stack([parts] * lax.axis_size(axes[k]))]
    transpose x1 -> x0, local copies, waits for them, and re-layouts: 9.88 us -> none  [all_blocks(): parts.transpose(*turned, *range(len(sequence), parts.ndim))]
  transfers between devices with their start and end apart: 8 -> 9, of which waited for: 7 -> 7; matrix products, arithmetic and copies ran while one was open for 29% -> 23% of each run, Pallas kernels for 0% -> 0%
where the time goes in v1:
time: 579 us; the launch traced here: 574 us
  waiting for transfers between devices  252 us (44%)
  matrix products  87.2 us (15%)
  local copies, waits for them, and re-layouts  70.3 us (12%)
  other arithmetic  64.2 us (11%)
  starting transfers between devices  45.3 us (8%)
  blocking collectives  40.7 us (7%)
  between operations  14.3 us (2%)
    all_to_all x3, waiting for transfers between devices, all_blocks(): lax.all_to_all(jnp.stack([parts] * lax.axis_size(axes[k])), axes[k], 0, 0)  149 us
    all_to_all x3, waiting for transfers between devices, sent_to_all(): return lax.all_to_all(copies, axis, split_axis=0, concat_axis=0, tiled=True)  83.4 us
    dot_general x17, matrix products, fold_block(): jnp.einsum(forms, weights.astype(jnp.bfloat16), value_block, preferred_el...  39.1 us
    all_gather x1, blocking collectives, in_one_piece_2(): out = lax.all_gather(both, axis, axis=dim, tiled=True)  30.6 us
    reduce_sum x17, other arithmetic, fold_block(): weight_sum = weight_sum * decay + jnp.sum(weights, axis=-1)  28 us
    dot_general x8, matrix products, make_advance(): jnp.einsum('qhd,khd->hqk', query_rows, key_block, preferred_element_type=...  22.5 us
    all_to_all x3, starting transfers between devices, sent_to_all(): return lax.all_to_all(copies, axis, split_axis=0, concat_axis=0, tiled=True)  17.9 us
    all_to_all x3, starting transfers between devices, all_blocks(): lax.all_to_all(jnp.stack([parts] * lax.axis_size(axes[k])), axes[k], 0, 0)  17 us
  transfers between devices with their start and end apart: 9, of which 7 were waited for; matrix products, arithmetic and copies ran while one was open for 23% of the time, Pallas kernels for 0%

profile of v1, /device:TPU:14, one launch (start us, length us, event | category | flops | bytes accessed | tf_op | source)
XLA Modules:
  0.0 574.3 jit_solution(14416532259944610113)
XLA Ops:
  6.5 3.0 reshape_squeeze.6
  11.7 6.3 %all-to-all-start = ((bf16[64,3,16,80]{3,0,1,2:T(8,128)(2,1)}), bf16[64,3,16,80]{3,0,1,2:T(8,128)(2,1)}, u32[]{:S(2)}, u32[]{:S(2)}) async-start(bf16[64,3,16,80]{3,0,1,2:T(8,128)(2,1)} %copy.153), calls=%async_computation | async-start | bytes 1572864 | tf_op jit(solution)/shard_map/all_to_all | solution.py:114
  20.0 8.9 %all-to-all-done = bf16[64,3,16,80]{3,0,1,2:T(8,128)(2,1)} async-done(((bf16[64,3,16,80]{3,0,1,2:T(8,128)(2,1)}), bf16[64,3,16,80]{3,0,1,2:T(8,128)(2,1)}, u32[]{:S(2)}, u32[]{:S(2)}) %all-to-all-start) | async-done | bytes 491552 | tf_op jit(solution)/shard_map/all_to_all | solution.py:114
  28.9 4.3 all-to-all-start.4
  33.2 2.3 copy.155
  35.6 2.5 all_to_all.49
  39.9 3.0 all-to-all-done.4
  42.9 2.8 broadcast_in_dim.145
  45.7 7.6 %all-to-all-start.1 = ((bf16[8,512,4,80]{1,3,2,0:T(8,128)(2,1)}), bf16[8,512,4,80]{1,3,2,0:T(8,128)(2,1)}, u32[]{:S(2)}, u32[]{:S(2)}) async-start(bf16[8,512,4,80]{1,3,2,0:T(8,128)(2,1)} %broadcast_in_dim.145), calls=%async_computation.1 | async-start | bytes 5242880 | tf_op jit(solution)/shard_map/all_to_all | solution.py:22
  53.3 61.6 %all-to-all-done.1 = bf16[8,512,4,80]{1,3,2,0:T(8,128)(2,1)} async-done(((bf16[8,512,4,80]{1,3,2,0:T(8,128)(2,1)}), bf16[8,512,4,80]{1,3,2,0:T(8,128)(2,1)}, u32[]{:S(2)}, u32[]{:S(2)}) %all-to-all-start.1) | async-done | bytes 2621472 | tf_op jit(solution)/shard_map/all_to_all | solution.py:22
  114.9 2.9 stack.10
  117.8 5.0 all-to-all-start.5
  126.9 76.7 %while.33 = (s32[]{:T(128)}, f32[2,512]{1,0:T(2,128)S(1)}, f32[2,512]{1,0:T(2,128)S(1)}, f32[2,512,80]{1,2,0:T(8,128)}, s32[8]{0:T(128)S(1)}, /*index=5*/s32[]{:...) while((s32[]{:T(128)}, f32[2,512]{1,0:T(2,128)S(1)}, ...), condition=%wide.region_5.6_spmd.clone, body=%wide.region_2.5_spmd.clone.sunk | while | flops 174861312 | bytes 15896233 | solution.py:146
  128.8 2.8 bitcast_reduce_fusion.5
  134.0 2.4 convolution_add_fusion.2
  138.3 2.8 bitcast_reduce_fusion.5
  143.5 2.5 convolution_add_fusion.2
  147.9 2.8 bitcast_reduce_fusion.5
  153.1 2.5 convolution_add_fusion.2
  157.5 2.8 bitcast_reduce_fusion.5
  162.7 2.5 convolution_add_fusion.2
  167.1 2.8 bitcast_reduce_fusion.5
  172.3 2.5 convolution_add_fusion.2
  176.7 2.8 bitcast_reduce_fusion.5
  181.9 2.5 convolution_add_fusion.2
  186.3 2.8 bitcast_reduce_fusion.5
  191.5 2.5 convolution_add_fusion.2
  195.9 2.8 bitcast_reduce_fusion.5
  201.1 2.5 convolution_add_fusion.2
  205.4 10.1 %all_to_all.69 = bf16[512,2,80]{2,1,0:T(2,128)(2,1)S(1)} all-to-all(bf16[512,2,80]{2,1,0:T(2,128)(2,1)} %bitcast.256), channel_id=1, replica_groups=mesh['img'=4,'seq_0'=2,'seq_1'=4,'tp'=8] {'seq_0','seq_1'}, dimensions={0} | all-to-all | bytes 327680 | tf_op jit(solution)/shard_map/all_to_all | solution.py:149
  215.6 7.1 %stack.11 = bf16[4,8,160,1024]{3,2,1,0:T(8,128)(2,1)} broadcast(bf16[8,160,1024]{2,1,0:T(8,128)(2,1)} %bitcast.38), dimensions={1,2,3} | broadcast | bytes 13107200 | tf_op jit(solution)/shard_map/stack | solution.py:49
  222.7 7.8 %all-to-all-start.6 = ((bf16[4,8,160,1024]{3,2,1,0:T(8,128)(2,1)}), bf16[4,8,160,1024]{3,2,1,0:T(8,128)(2,1)}, u32[]{:S(2)}, u32[]{:S(2)}) async-start(bf16[4,8,160,1024]{3,2,1,0:T(8,128)(2,1)} %stack.11), calls=%async_computation.6 | async-start | bytes 20971520 | tf_op jit(solution)/shard_map/all_to_all | solution.py:49
  237.2 146.2 %all-to-all-done.6 = bf16[4,8,160,1024]{3,2,1,0:T(8,128)(2,1)} async-done(((bf16[4,8,160,1024]{3,2,1,0:T(8,128)(2,1)}), bf16[4,8,160,1024]{3,2,1,0:T(8,128)(2,1)}, u32[]{:S(2)}, u32[]{:S(2)}) %all-to-all-start.6) | async-done | bytes 10485792 | tf_op jit(solution)/shard_map/all_to_all | solution.py:49
  384.6 7.1 %all-to-all-start.3 = ((bf16[8,16,5120]{2,1,0:T(8,128)(2,1)}), bf16[8,16,5120]{2,1,0:T(8,128)(2,1)S(1)}, u32[]{:S(2)}, u32[]{:S(2)}) async-start(bf16[8,16,5120]{2,1,0:T(8,128)(2,1)} %broadcast_in_dim.147), calls=%async_computation.3 | async-start | bytes 2621440 | tf_op jit(solution)/shard_map/all_to_all | solution.py:22
  392.9 4.9 fusion.55
  397.8 9.8 %copy.164 = bf16[4,8,160,1024]{3,2,0,1:T(8,128)(2,1)} copy(bf16[4,8,160,1024]{3,2,1,0:T(8,128)(2,1)} %all-to-all-done.6) | data formatting | bytes 20971520 | tf_op jit(solution)/shard_map/all_to_all | solution.py:49
  407.6 18.8 %all-to-all-done.3 = bf16[8,16,5120]{2,1,0:T(8,128)(2,1)S(1)} async-done(((bf16[8,16,5120]{2,1,0:T(8,128)(2,1)}), bf16[8,16,5120]{2,1,0:T(8,128)(2,1)S(1)}, u32[]{:S(2)}, u32[]{:S(2)}) %all-to-all-start.3) | async-done | bytes 1310752 | tf_op jit(solution)/shard_map/all_to_all | solution.py:22
  426.4 5.5 convolution_convert_fusion.1
  432.7 3.3 all-to-all-start.7
  436.0 4.5 fusion.57
  440.5 3.0 all-to-all-done.7
  443.6 3.7 fusion.65
  448.6 4.1 all-to-all-start.8
  454.0 7.4 %add_bitcast_fusion = f32[1,8,512,128]{3,2,1,0:T(8,128)} fusion(f32[512,512,8]{1,0,2:T(8,128)} %get-tuple-element.412, f32[8,512]{1,0:T(8,128)S(1)} %get-tuple-element.408, pred[512,512]{0,1:T(8,128)(4,1)S(1)} %iota_compare_fusion, f32[8,512]{1,0:T(8,128)S(1)} %get-tuple-element.406, bf16[1,512,1,1,128]{4,2,3,1,0:T(2,128)(2,1)S(1)} %copy-done.8), kind=kOutput, calls=%fused_computation.94 | convolution fusion | flops 547880960 | bytes 10911744 | tf_op jit(solution)/shard_map/kgcn,nkd->kgcd/dot_general | solution.py:90
  461.4 9.4 %all-to-all-done.8 = bf16[8,128,2,1,128]{4,2,1,3,0:T(2,128)(2,1)S(1)} async-done(((bf16[8,128,2,1,128]{4,2,1,3,0:T(2,128)(2,1)}), bf16[8,128,2,1,128]{4,2,1,3,0:T(2,128)(2,1)S(1)}, u32[]{:S(2)}, u32[]{:S(2)}) %all-to-all-start.8) | async-done | bytes 524320 | tf_op jit(solution)/shard_map/all_to_all | solution.py:72
  471.5 30.6 %all_gather.7 = bf16[1024,2,128]{2,0,1:T(8,128)(2,1)S(1)} all-gather(bf16[128,2,128]{2,0,1:T(8,128)(2,1)S(1)} %pad_maximum_fusion.2), channel_id=1, replica_groups=mesh['img'=4,'seq_0'=2,'seq_1'=4,'tp'=8] {'seq_0','seq_1'}, dimensions={0}, use_global_device_ids=true | all-gather | bytes 589824 | tf_op jit(solution)/shard_map/all_gather | solution.py:79
  502.8 59.9 %while.32 = (s32[]{:T(128)}, f32[1,8,512]{2,1,0:T(8,128)S(1)}, f32[1,8,512]{2,1,0:T(8,128)}, f32[1,8,512,128]{3,2,1,0:T(8,128)}, s32[8]{0:T(128)}, /*index=5*/s3...) while((s32[]{:T(128)}, f32[1,8,512]{2,1,0:T(8,128)S(1)}, ...), condition=%wide.region_14.15_spmd, body=%wide.region_11.14_spmd.sunk | while | flops 276312320 | bytes 28641332 | solution.py:223
  563.7 3.8 fusion.68
  (223 shorter events, 119.9 us)
Async XLA Ops:
  6.5 228.5 %copy-start = (bf16[1280,1280]{1,0:T(8,128)(2,1)S(1)}, bf16[1280,1280]{1,0:T(8,128)(2,1)}, u32[]{:S(2)}) copy-start(bf16[1280,1280]{1,0:T(8,128)(2,1)} %param.15) | copy-start | bytes 9830404
  11.7 17.2 %all-to-all-start = ((bf16[64,3,16,80]{3,0,1,2:T(8,128)(2,1)}), bf16[64,3,16,80]{3,0,1,2:T(8,128)(2,1)}, u32[]{:S(2)}, u32[]{:S(2)}) async-start(bf16[64,3,16,80]{3,0,1,2:T(8,128)(2,1)} %copy.153), calls=%async_computation | async-start | bytes 1572864 | tf_op jit(solution)/shard_map/all_to_all | solution.py:114
  28.9 13.9 %all-to-all-start.4 = ((bf16[2,1,160,1024]{3,2,1,0:T(8,128)(2,1)}), bf16[2,1,160,1024]{3,2,1,0:T(8,128)(2,1)}, u32[]{:S(2)}, u32[]{:S(2)}) async-start(bf16[2,1,160,1024]{3,2,1,0:T(8,128)(2,1)} %pad_maximum_fusion), calls=%async_computation.4 | async-start | bytes 1310720 | tf_op jit(solution)/shard_map/all_to_all | solution.py:49
  45.7 69.2 %all-to-all-start.1 = ((bf16[8,512,4,80]{1,3,2,0:T(8,128)(2,1)}), bf16[8,512,4,80]{1,3,2,0:T(8,128)(2,1)}, u32[]{:S(2)}, u32[]{:S(2)}) async-start(bf16[8,512,4,80]{1,3,2,0:T(8,128)(2,1)} %broadcast_in_dim.145), calls=%async_computation.1 | async-start | bytes 5242880 | tf_op jit(solution)/shard_map/all_to_all | solution.py:22
  117.8 87.6 %all-to-all-start.5 = ((bf16[4,2,160,1024]{3,2,1,0:T(8,128)(2,1)}), bf16[4,2,160,1024]{3,2,1,0:T(8,128)(2,1)}, u32[]{:S(2)}, u32[]{:S(2)}) async-start(bf16[4,2,160,1024]{3,2,1,0:T(8,128)(2,1)} %stack.10), calls=%async_computation.5 | async-start | bytes 5242880 | tf_op jit(solution)/shard_map/all_to_all | solution.py:49
  131.6 2.4 copy-start.2
  141.1 2.4 copy-start.2
  150.7 2.4 copy-start.2
  160.3 2.4 copy-start.2
  169.9 2.4 copy-start.2
  179.5 2.4 copy-start.2
  189.1 2.4 copy-start.2
  198.7 2.4 copy-start.2
  222.7 160.8 %all-to-all-start.6 = ((bf16[4,8,160,1024]{3,2,1,0:T(8,128)(2,1)}), bf16[4,8,160,1024]{3,2,1,0:T(8,128)(2,1)}, u32[]{:S(2)}, u32[]{:S(2)}) async-start(bf16[4,8,160,1024]{3,2,1,0:T(8,128)(2,1)} %stack.11), calls=%async_computation.6 | async-start | bytes 20971520 | tf_op jit(solution)/shard_map/all_to_all | solution.py:49
  230.4 213.1 %all-gather.2.cloned.1.call-start = ((), (), s32[]{:S(2)}) async-start(), calls=%async_computation.9 | async-start | bytes 4325376 | tf_op jit(solution)/shard_map/all_gather | solution.py:180
  235.0 2.0 copy-start.9
  237.2 154.6 %copy-start.7 = (bf16[1,512,2,1,128]{4,2,3,1,0:T(2,128)(2,1)S(1)}, bf16[1,512,2,1,128]{4,2,3,1,0:T(2,128)(2,1)}, u32[]{:S(2)}) copy-start(bf16[1,512,2,1,128]{4,2,3,1,0:T(2,128)(2,1)} %param.21) | copy-start | bytes 786436
  384.6 8.2 %copy-start.5 = (bf16[1,512,8,128]{3,2,1,0:T(8,128)(2,1)S(1)}, bf16[1,512,8,128]{3,2,1,0:T(8,128)(2,1)}, u32[]{:S(2)}) copy-start(bf16[1,512,8,128]{3,2,1,0:T(8,128)(2,1)} %param.20) | copy-start | bytes 3145732
  384.6 41.8 %all-to-all-start.3 = ((bf16[8,16,5120]{2,1,0:T(8,128)(2,1)}), bf16[8,16,5120]{2,1,0:T(8,128)(2,1)S(1)}, u32[]{:S(2)}, u32[]{:S(2)}) async-start(bf16[8,16,5120]{2,1,0:T(8,128)(2,1)} %broadcast_in_dim.147), calls=%async_computation.3 | async-start | bytes 2621440 | tf_op jit(solution)/shard_map/all_to_all | solution.py:22
  432.7 10.9 %all-to-all-start.7 = ((f32[8,1,128]{2,1,0:T(1,128)}), f32[8,1,128]{2,1,0:T(1,128)S(1)}, u32[]{:S(2)}, u32[]{:S(2)}) async-start(f32[8,1,128]{2,1,0:T(1,128)} %broadcast_in_dim.148), calls=%async_computation.7 | async-start | bytes 8192 | tf_op jit(solution)/shard_map/all_to_all | solution.py:22
  436.0 7.6 %copy-start.10 = (f32[1024]{0:T(1024)S(1)}, f32[1024]{0:T(1024)}, u32[]{:S(2)}) copy-start(f32[1024]{0:T(1024)} %param.18) | copy-start | bytes 12292
  447.3 6.1 %copy-start.6 = (bf16[1,512,8,128]{3,2,1,0:T(8,128)(2,1)S(1)}, bf16[1,512,8,128]{3,2,1,0:T(8,128)(2,1)}, u32[]{:S(2)}) copy-start(bf16[1,512,8,128]{3,2,1,0:T(8,128)(2,1)} %param.20) | copy-start | bytes 3145732
  447.4 6.6 %copy-start.8 = (bf16[1,512,1,1,128]{4,2,3,1,0:T(2,128)(2,1)S(1)}, bf16[1,512,1,1,128]{4,2,3,1,0:T(2,128)(2,1)}, u32[]{:S(2)}) copy-start(bf16[1,512,1,1,128]{4,2,3,1,0:T(2,128)(2,1)} %get-tuple-element.402) | copy-start | bytes 393220
  448.6 22.2 %all-to-all-start.8 = ((bf16[8,128,2,1,128]{4,2,1,3,0:T(2,128)(2,1)}), bf16[8,128,2,1,128]{4,2,1,3,0:T(2,128)(2,1)S(1)}, u32[]{:S(2)}, u32[]{:S(2)}) async-start(bf16[8,128,2,1,128]{4,2,1,3,0:T(2,128)(2,1)} %bitcast.192), calls=%async_computation.8 | async-start | bytes 1048576 | tf_op jit(solution)/shard_map/all_to_all | solution.py:72
  502.8 3.3 copy-start.3
  507.7 1.3 copy-start.4
  510.3 3.3 copy-start.3
  515.1 1.3 copy-start.4
  517.8 3.3 copy-start.3
  522.6 1.3 copy-start.4
  525.3 3.3 copy-start.3
  530.1 1.3 copy-start.4
  532.8 3.3 copy-start.3
  537.6 1.3 copy-start.4
  540.3 3.3 copy-start.3
  545.1 1.3 copy-start.4
  547.8 3.3 copy-start.3
  552.6 1.3 copy-start.4
  555.2 3.3 copy-start.3
  560.1 1.3 copy-start.4
  562.7 4.8 copy-start.1
Sparse Core Ops, SparseCore 0:
  233.0 156.4 all-gather.1
